TPU v7x, 32 devices: a whole 2x2x4 slice. The times are simulated.
32 devices in a mesh: tm: 2 (over x), lat: 4 (over y, core), lon: 4 (over z).
Axes of the slice: x: 2, y: 2, z: 4, core: 2. Of those that a mesh axis runs over, the one named last changes fastest.
Arguments:
- forcing: float32 [8, 512, 2048], P('tm', 'lat', 'lon'), may hold values from -17 to 17
- depth: float32 [512, 2048], P('lat', 'lon'), may hold values from 0.2 to 2
- mask: int32 [512, 2048], P('lat', 'lon'), may hold values 0 or 1
- guess: float32 [2, 512, 2048], P('tm', 'lat', 'lon'), may hold values from -6 to 6
Outputs:
- adjoint: float32 [8, 512, 2048], P('tm', 'lat', 'lon')
All inputs are finite; a program needn't handle non-finite values. No bound on the sum of `mask` on one device may be relied on, other than what follows from the above.
Results may differ from a plain program's by a relative error of at most 0.0001.
Values sent between devices are 32-bit elements; how exact they have to be, the bound alone decides.
No kernel may reach another device: no remote copies, remote signals or barrier semaphores. Data moves between devices by JAX's collectives and lax.ppermute only.
A program may use at most 64 MiB of HBM per device.

v0:
```python
import jax
import jax.numpy as jnp
from jax import lax
from jax.sharding import PartitionSpec as P

FS = 4
FINE_ITERS = 2
COUPLING = 3.0
EPSILON = 1e-06


def with_halo(block, sides, width):
    for axis, dim in sides:
        count = lax.axis_size(axis)
        forward = [(i, i + 1) for i in range(count - 1)]
        forward.append((count - 1, 0))
        backward = [(target, source) for source, target in forward]
        low = lax.ppermute(
            lax.slice_in_dim(block, block.shape[dim] - width, None, axis=dim), axis, forward
        )
        high = lax.ppermute(lax.slice_in_dim(block, 0, width, axis=dim), axis, backward)
        block = jnp.concatenate([low, block, high], axis=dim)
    return block


def shifted(array, axis, by):
    size = lax.axis_size(axis)
    pairs = [(i, i + by) for i in range(size) if 0 <= i + by < size]
    return lax.ppermute(array, axis, pairs)


def face_terms(depth, mask):
    wet = mask.astype(jnp.float32)
    stacked = jnp.stack([wet, depth])
    padded = with_halo(stacked, (("lat", 1), ("lon", 2)), 1)
    rows = depth.shape[0]
    wet_pad = padded[0]
    deep_pad = padded[1]
    middle_wet = wet_pad[1:-1]
    middle_deep = deep_pad[1:-1]
    across = (
        COUPLING
        * middle_wet[:, :-1]
        * middle_wet[:, 1:]
        * 0.5
        * (middle_deep[:, :-1] + middle_deep[:, 1:])
    )
    along = (
        COUPLING
        * wet_pad[:-1, 1:-1]
        * wet_pad[1:, 1:-1]
        * 0.5
        * (deep_pad[:-1, 1:-1] + deep_pad[1:, 1:-1])
    )
    first = lax.axis_index("lat") == 0
    final = lax.axis_index("lat") == lax.axis_size("lat") - 1
    face_row = lax.broadcasted_iota(jnp.int32, along.shape, 0)
    along = jnp.where(first & (face_row == 0) | final & (face_row == rows), 0.0, along)
    return (across[:, 1:], across[:, :-1], along[1:], along[:-1])


def apply_op(field, faces, factor):
    east, west, north, south = faces
    padded = with_halo(field, (("lat", 0), ("lon", 1)), 1)
    spread = east * (field - padded[1:-1, 2:]) + west * (field - padded[1:-1, :-2])
    spread = spread + north * (field - padded[2:, 1:-1]) + south * (field - padded[:-2, 1:-1])
    return field + factor * spread


def paired(residual, image):
    return lax.psum((jnp.sum(residual * residual), jnp.sum(residual * image)), ("lat", "lon"))


def fine_solve(source, faces):
    solution = jnp.zeros_like(source)
    residual = source
    direction = source
    image = apply_op(source, faces, 1.0)
    norm_now, product = paired(source, image)
    alpha = norm_now / (product + EPSILON)
    along = image
    for level in range(FINE_ITERS):
        solution = solution + alpha * direction
        residual = residual - alpha * along
        if level + 1 < FINE_ITERS:
            image = apply_op(residual, faces, 1.0)
            norm_next, product = paired(residual, image)
            ratio = norm_next / (norm_now + EPSILON)
            alpha = norm_next / (product - ratio * norm_next / alpha + EPSILON)
            direction = residual + ratio * direction
            along = image + ratio * along
            norm_now = norm_next
    return solution


def coarse_solve(source, faces):
    image = apply_op(source, faces, float(FS))
    norm_now, product = lax.psum(
        (jnp.sum(source * source), jnp.sum(source * image)), ("lat", "lon")
    )
    return norm_now / (product + EPSILON) * source


def local(forcing, depth, mask, guess):
    faces = face_terms(depth, mask)
    start = guess[0]
    value = start
    for level in range(FS - 1, 0, -1):
        value = fine_solve(value, faces) + forcing[level]
    finished = fine_solve(value, faces) + forcing[0]
    offset = finished - coarse_solve(start, faces)
    position = lax.axis_index("tm")
    slab_count = lax.axis_size("tm")
    is_final = position == slab_count - 1

    def turn(index, upper):
        here = coarse_solve(upper, faces) + offset
        moved = shifted(here, "tm", -1)
        return jnp.where(is_final, start, moved)

    upper = lax.fori_loop(0, slab_count - 1, turn, start)
    here = coarse_solve(upper, faces) + offset
    value = upper
    later = []
    for level in range(FS - 1, 0, -1):
        value = fine_solve(value, faces) + forcing[level]
        later.append(value)
    return jnp.stack([here] + later[::-1])


def solution(mesh):
    return jax.shard_map(
        local,
        mesh=mesh,
        in_specs=(P("tm", "lat", "lon"), P("lat", "lon"), P("lat", "lon"), P("tm", "lat", "lon")),
        out_specs=P("tm", "lat", "lon"),
        check_vma=False,
    )
```

profile of v0, /device:TPU:0, one launch (start us, length us, event | category | flops | bytes accessed | tf_op | source)
XLA Modules:
  0.0 654.5 jit_solution(5138492691054062486)
XLA Ops:
  1.6 2.0 collective-permute-start.1
  5.6 2.4 collective-permute-start.2
  7.9 2.1 collective-permute-start.3
  10.1 2.0 collective-permute-start.6
  12.2 1.7 collective-permute-done.2
  13.9 3.4 collective-permute-done.3
  20.8 31.9 %all-reduce.13 = (f32[]{:T(128)}, f32[]{:T(128)}) all-reduce(f32[]{:T(128)} %get-tuple-element.47, f32[]{:T(128)} %get-tuple-element.22), channel_id=1, replica_groups=mesh['tm'=2,'lat'=4,'lon'=4] {'lat','lon'}, use_global_device_ids=true, to_apply=%region_1.2 | all-reduce | flops 2 | bytes 16 | tf_op jit(solution)/shard_map/while/body/eval_jaxpr/psum | solution.py:98
  54.2 1.7 collective-permute-start.9
  57.4 2.0 collective-permute-start.11
  61.7 2.0 collective-permute-done.11
  64.6 31.9 %all-reduce.12 = (f32[]{:T(128)}, f32[]{:T(128)}) all-reduce(f32[]{:T(128)} %get-tuple-element.61, f32[]{:T(128)} %get-tuple-element.60), channel_id=1, replica_groups=mesh['tm'=2,'lat'=4,'lon'=4] {'lat','lon'}, use_global_device_ids=true, to_apply=%region_7.8 | all-reduce | flops 2 | bytes 16 | tf_op jit(solution)/shard_map/psum | solution.py:71
  99.9 1.7 collective-permute-start.13
  103.1 2.0 collective-permute-start.15
  105.2 2.7 collective-permute-done.14
  110.5 32.1 %all-reduce.11 = (f32[]{:T(128)}, f32[]{:T(128)}) all-reduce(f32[]{:T(128)} %get-tuple-element.59, f32[]{:T(128)} %get-tuple-element.58), channel_id=1, replica_groups=mesh['tm'=2,'lat'=4,'lon'=4] {'lat','lon'}, use_global_device_ids=true, to_apply=%region_11.12 | all-reduce | flops 2 | bytes 16 | tf_op jit(solution)/shard_map/psum | solution.py:71
  143.8 1.7 collective-permute-start.17
  147.0 2.0 collective-permute-start.19
  149.6 2.4 collective-permute-done.18
  152.1 1.9 collective-permute-done.19
  154.9 31.1 %all-reduce.10 = (f32[]{:T(128)}, f32[]{:T(128)}) all-reduce(f32[]{:T(128)} %get-tuple-element.57, f32[]{:T(128)} %get-tuple-element.56), channel_id=1, replica_groups=mesh['tm'=2,'lat'=4,'lon'=4] {'lat','lon'}, use_global_device_ids=true, to_apply=%region_15.16 | all-reduce | flops 2 | bytes 16 | tf_op jit(solution)/shard_map/psum | solution.py:71
  189.2 1.7 collective-permute-start.21
  194.4 2.7 collective-permute-done.22
  197.1 2.8 collective-permute-done.23
  200.9 32.0 %all-reduce.9 = (f32[]{:T(128)}, f32[]{:T(128)}) all-reduce(f32[]{:T(128)} %get-tuple-element.55, f32[]{:T(128)} %get-tuple-element.54), channel_id=1, replica_groups=mesh['tm'=2,'lat'=4,'lon'=4] {'lat','lon'}, use_global_device_ids=true, to_apply=%region_19.20 | all-reduce | flops 2 | bytes 16 | tf_op jit(solution)/shard_map/psum | solution.py:71
  234.2 1.7 collective-permute-start.25
  237.4 2.0 collective-permute-start.27
  240.0 2.4 collective-permute-done.26
  242.4 1.9 collective-permute-done.27
  245.3 31.3 %all-reduce.8 = (f32[]{:T(128)}, f32[]{:T(128)}) all-reduce(f32[]{:T(128)} %get-tuple-element.53, f32[]{:T(128)} %get-tuple-element.52), channel_id=1, replica_groups=mesh['tm'=2,'lat'=4,'lon'=4] {'lat','lon'}, use_global_device_ids=true, to_apply=%region_23.24 | all-reduce | flops 2 | bytes 16 | tf_op jit(solution)/shard_map/psum | solution.py:71
  279.8 1.7 collective-permute-start.29
  285.0 2.6 collective-permute-done.30
  287.6 2.5 collective-permute-done.31
  291.1 31.6 %all-reduce.7 = (f32[]{:T(128)}, f32[]{:T(128)}) all-reduce(f32[]{:T(128)} %get-tuple-element.51, f32[]{:T(128)} %get-tuple-element.50), channel_id=1, replica_groups=mesh['tm'=2,'lat'=4,'lon'=4] {'lat','lon'}, use_global_device_ids=true, to_apply=%region_27.28 | all-reduce | flops 2 | bytes 16 | tf_op jit(solution)/shard_map/psum | solution.py:71
  323.9 1.7 collective-permute-start.33
  327.2 2.0 collective-permute-start.35
  329.7 2.2 collective-permute-done.34
  331.9 1.9 collective-permute-done.35
  334.8 32.4 %all-reduce.6 = (f32[]{:T(128)}, f32[]{:T(128)}, f32[]{:T(128)}) all-reduce(f32[]{:T(128)} %get-tuple-element.49, f32[]{:T(128)} %get-tuple-element.48, f32[]{:T(128)} %get-tuple-element.21), channel_id=1, replica_groups=mesh['tm'=2,'lat'=4,'lon'=4] {'lat','lon'}, use_global_device_ids=true, to_apply=%region_31.32 | all-reduce | flops 3 | bytes 24 | tf_op jit(solution)/shard_map/psum | solution.py:71
  373.1 7.0 %collective-permute-done.36 = f32[128,512]{1,0:T(8,128)S(1)} collective-permute-done((f32[128,512]{1,0:T(8,128)S(1)}, f32[128,512]{1,0:T(8,128)S(1)}, u32[]{:S(2)}, u32[]{:S(2)}) %collective-permute-start.36) | collective-permute-done | bytes 262176 | tf_op jit(solution)/shard_map/while/body/eval_jaxpr/ppermute | solution.py:29
  380.1 1.7 collective-permute-start.38
  385.4 2.9 collective-permute-done.39
  388.3 3.0 collective-permute-done.40
  392.2 30.8 %all-reduce.5 = (f32[]{:T(128)}, f32[]{:T(128)}) all-reduce(f32[]{:T(128)} %get-tuple-element.25, f32[]{:T(128)} %get-tuple-element.24), channel_id=1, replica_groups=mesh['tm'=2,'lat'=4,'lon'=4] {'lat','lon'}, use_global_device_ids=true, to_apply=%region_35.36 | all-reduce | flops 2 | bytes 16 | tf_op jit(solution)/shard_map/psum | solution.py:98
  424.4 1.7 collective-permute-start.42
  430.4 1.9 collective-permute-done.43
  432.3 3.2 collective-permute-done.44
  436.4 32.0 %all-reduce.4 = (f32[]{:T(128)}, f32[]{:T(128)}) all-reduce(f32[]{:T(128)} %get-tuple-element.46, f32[]{:T(128)} %get-tuple-element.45), channel_id=1, replica_groups=mesh['tm'=2,'lat'=4,'lon'=4] {'lat','lon'}, use_global_device_ids=true, to_apply=%region_41.42 | all-reduce | flops 2 | bytes 16 | tf_op jit(solution)/shard_map/psum | solution.py:71
  472.1 1.7 collective-permute-start.46
  475.3 2.0 collective-permute-start.48
  477.3 3.0 collective-permute-done.47
  480.3 1.9 collective-permute-done.48
  483.1 31.3 %all-reduce.3 = (f32[]{:T(128)}, f32[]{:T(128)}) all-reduce(f32[]{:T(128)} %get-tuple-element.44, f32[]{:T(128)} %get-tuple-element.43), channel_id=1, replica_groups=mesh['tm'=2,'lat'=4,'lon'=4] {'lat','lon'}, use_global_device_ids=true, to_apply=%region_45.46 | all-reduce | flops 2 | bytes 16 | tf_op jit(solution)/shard_map/psum | solution.py:71
  515.8 1.7 collective-permute-start.50
  521.5 2.1 collective-permute-done.51
  523.7 2.5 collective-permute-done.52
  527.1 31.3 %all-reduce.2 = (f32[]{:T(128)}, f32[]{:T(128)}) all-reduce(f32[]{:T(128)} %get-tuple-element.42, f32[]{:T(128)} %get-tuple-element.41), channel_id=1, replica_groups=mesh['tm'=2,'lat'=4,'lon'=4] {'lat','lon'}, use_global_device_ids=true, to_apply=%region_49.50 | all-reduce | flops 2 | bytes 16 | tf_op jit(solution)/shard_map/psum | solution.py:71
  561.8 1.7 collective-permute-start.54
  567.0 2.8 collective-permute-done.55
  569.8 2.4 collective-permute-done.56
  573.2 31.8 %all-reduce.1 = (f32[]{:T(128)}, f32[]{:T(128)}) all-reduce(f32[]{:T(128)} %get-tuple-element.40, f32[]{:T(128)} %get-tuple-element.38), channel_id=1, replica_groups=mesh['tm'=2,'lat'=4,'lon'=4] {'lat','lon'}, use_global_device_ids=true, to_apply=%region_53.54 | all-reduce | flops 2 | bytes 16 | tf_op jit(solution)/shard_map/psum | solution.py:71
  609.4 2.0 collective-permute-start.60
  612.0 2.2 collective-permute-done.59
  614.2 1.9 collective-permute-done.60
  617.0 31.8 %all-reduce = (f32[]{:T(128)}, f32[]{:T(128)}, f32[]{:T(128)}) all-reduce(f32[]{:T(128)} %get-tuple-element.36, f32[]{:T(128)} %get-tuple-element.26, f32[]{:T(128)} %get-tuple-element.23), channel_id=1, replica_groups=mesh['tm'=2,'lat'=4,'lon'=4] {'lat','lon'}, use_global_device_ids=true, to_apply=%region_57.58 | all-reduce | flops 3 | bytes 24 | tf_op jit(solution)/shard_map/psum | solution.py:71
  (145 shorter events, 59.8 us)
Async XLA Ops:
  0.0 1.0 copy-start.2
  1.0 2.6 copy-start
  1.1 4.4 collective-permute-start
  1.6 3.8 collective-permute-start.1
  3.6 6.4 collective-permute-start.4
  4.3 5.7 collective-permute-start.5
  5.6 8.4 %collective-permute-start.2 = (f32[2,130,1]{2,1,0:T(8,128)S(1)}, f32[2,130,1]{2,1,0:T(8,128)S(1)}, u32[]{:S(2)}, u32[]{:S(2)}) collective-permute-start(f32[2,130,1]{2,1,0:T(8,128)S(1)} %get-tuple-element.105), channel_id=1, source_target_pairs={{0,1},{1,2},{2,3},{3,0},{4,5},{5,6},{6,7},{7,4},{8,9},{9,10},{10,1... | collective-permute-start | bytes 3128 | tf_op jit(solution)/shard_map/ppermute | solution.py:18
  7.9 9.4 %collective-permute-start.3 = (f32[2,130,1]{2,1,0:T(8,128)S(1)}, f32[2,130,1]{2,1,0:T(8,128)S(1)}, u32[]{:S(2)}, u32[]{:S(2)}) collective-permute-start(f32[2,130,1]{2,1,0:T(8,128)S(1)} %get-tuple-element.106), channel_id=1, source_target_pairs={{1,0},{2,1},{3,2},{0,3},{5,4},{6,5},{7,6},{4,7},{9,8},{10,9},{11,1... | collective-permute-start | bytes 3128 | tf_op jit(solution)/shard_map/ppermute | solution.py:21
  10.1 9.2 %collective-permute-start.6 = (f32[130,1]{1,0:T(8,128)S(1)}, f32[130,1]{1,0:T(8,128)S(1)}, u32[]{:S(2)}, u32[]{:S(2)}) collective-permute-start(f32[130,1]{1,0:T(8,128)S(1)} %get-tuple-element.135), channel_id=1, source_target_pairs={{1,0},{2,1},{3,2},{0,3},{5,4},{6,5},{7,6},{4,7},{9,8},{10,9},{11,1... | collective-permute-start | bytes 1568 | tf_op jit(solution)/shard_map/while/body/eval_jaxpr/ppermute | solution.py:21
  12.1 7.7 %collective-permute-start.7 = (f32[130,1]{1,0:T(8,128)S(1)}, f32[130,1]{1,0:T(8,128)S(1)}, u32[]{:S(2)}, u32[]{:S(2)}) collective-permute-start(f32[130,1]{1,0:T(8,128)S(1)} %get-tuple-element.136), channel_id=1, source_target_pairs={{0,1},{1,2},{2,3},{3,0},{4,5},{5,6},{6,7},{7,4},{8,9},{9,10},{10,1... | collective-permute-start | bytes 1568 | tf_op jit(solution)/shard_map/while/body/eval_jaxpr/ppermute | solution.py:18
  54.1 45.7 %copy-start.1 = (f32[4,128,512]{2,1,0:T(8,128)S(1)}, f32[4,128,512]{2,1,0:T(8,128)}, u32[]{:S(2)}) copy-start(f32[4,128,512]{2,1,0:T(8,128)} %param.4) | copy-start | bytes 3145732
  54.1 3.1 collective-permute-start.8
  54.2 3.0 collective-permute-start.9
  57.3 4.4 collective-permute-start.10
  57.4 6.3 collective-permute-start.11
  99.9 3.1 collective-permute-start.12
  99.9 3.0 collective-permute-start.13
  103.1 4.8 collective-permute-start.14
  103.1 6.4 collective-permute-start.15
  143.8 3.1 collective-permute-start.16
  143.8 3.0 collective-permute-start.17
  147.0 5.1 collective-permute-start.18
  147.0 6.9 %collective-permute-start.19 = (f32[130,1]{1,0:T(8,128)S(1)}, f32[130,1]{1,0:T(8,128)S(1)}, u32[]{:S(2)}, u32[]{:S(2)}) collective-permute-start(f32[130,1]{1,0:T(8,128)S(1)} %get-tuple-element.130), channel_id=1, source_target_pairs={{0,1},{1,2},{2,3},{3,0},{4,5},{5,6},{6,7},{7,4},{8,9},{9,10},{10,1... | collective-permute-start | bytes 1568 | tf_op jit(solution)/shard_map/ppermute | solution.py:18
  189.2 3.1 collective-permute-start.20
  189.2 3.0 collective-permute-start.21
  192.4 4.7 collective-permute-start.22
  193.0 7.0 %collective-permute-start.23 = (f32[130,1]{1,0:T(8,128)S(1)}, f32[130,1]{1,0:T(8,128)S(1)}, u32[]{:S(2)}, u32[]{:S(2)}) collective-permute-start(f32[130,1]{1,0:T(8,128)S(1)} %get-tuple-element.128), channel_id=1, source_target_pairs={{0,1},{1,2},{2,3},{3,0},{4,5},{5,6},{6,7},{7,4},{8,9},{9,10},{10,1... | collective-permute-start | bytes 1568 | tf_op jit(solution)/shard_map/ppermute | solution.py:18
  234.1 3.1 collective-permute-start.24
  234.2 3.0 collective-permute-start.25
  237.3 5.1 collective-permute-start.26
  237.4 6.9 %collective-permute-start.27 = (f32[130,1]{1,0:T(8,128)S(1)}, f32[130,1]{1,0:T(8,128)S(1)}, u32[]{:S(2)}, u32[]{:S(2)}) collective-permute-start(f32[130,1]{1,0:T(8,128)S(1)} %get-tuple-element.126), channel_id=1, source_target_pairs={{0,1},{1,2},{2,3},{3,0},{4,5},{5,6},{6,7},{7,4},{8,9},{9,10},{10,1... | collective-permute-start | bytes 1568 | tf_op jit(solution)/shard_map/ppermute | solution.py:18
  279.8 3.1 collective-permute-start.28
  279.8 3.0 collective-permute-start.29
  283.0 4.6 collective-permute-start.30
  283.4 6.7 %collective-permute-start.31 = (f32[130,1]{1,0:T(8,128)S(1)}, f32[130,1]{1,0:T(8,128)S(1)}, u32[]{:S(2)}, u32[]{:S(2)}) collective-permute-start(f32[130,1]{1,0:T(8,128)S(1)} %get-tuple-element.124), channel_id=1, source_target_pairs={{0,1},{1,2},{2,3},{3,0},{4,5},{5,6},{6,7},{7,4},{8,9},{9,10},{10,1... | collective-permute-start | bytes 1568 | tf_op jit(solution)/shard_map/ppermute | solution.py:18
  323.9 3.1 collective-permute-start.32
  323.9 3.0 collective-permute-start.33
  327.1 4.8 collective-permute-start.34
  327.2 6.6 %collective-permute-start.35 = (f32[130,1]{1,0:T(8,128)S(1)}, f32[130,1]{1,0:T(8,128)S(1)}, u32[]{:S(2)}, u32[]{:S(2)}) collective-permute-start(f32[130,1]{1,0:T(8,128)S(1)} %get-tuple-element.122), channel_id=1, source_target_pairs={{0,1},{1,2},{2,3},{3,0},{4,5},{5,6},{6,7},{7,4},{8,9},{9,10},{10,1... | collective-permute-start | bytes 1568 | tf_op jit(solution)/shard_map/ppermute | solution.py:18
  371.8 8.3 %collective-permute-start.36 = (f32[128,512]{1,0:T(8,128)S(1)}, f32[128,512]{1,0:T(8,128)S(1)}, u32[]{:S(2)}, u32[]{:S(2)}) collective-permute-start(f32[128,512]{1,0:T(8,128)S(1)} %get-tuple-element.95), channel_id=1, source_target_pairs={{16,0},{17,1},{18,2},{19,3},{20,4},{21,5},{22,6},{23,7},{24,8},{25... | collective-permute-start | bytes 786440 | tf_op jit(solution)/shard_map/while/body/eval_jaxpr/ppermute | solution.py:29
  380.1 3.1 collective-permute-start.37
  380.1 3.0 collective-permute-start.38
  383.3 5.0 collective-permute-start.39
  384.8 6.5 collective-permute-start.40
  424.4 3.1 collective-permute-start.41
  424.4 3.0 collective-permute-start.42
  427.6 4.7 collective-permute-start.43
  428.6 6.9 %collective-permute-start.44 = (f32[130,1]{1,0:T(8,128)S(1)}, f32[130,1]{1,0:T(8,128)S(1)}, u32[]{:S(2)}, u32[]{:S(2)}) collective-permute-start(f32[130,1]{1,0:T(8,128)S(1)} %get-tuple-element.118), channel_id=1, source_target_pairs={{0,1},{1,2},{2,3},{3,0},{4,5},{5,6},{6,7},{7,4},{8,9},{9,10},{10,1... | collective-permute-start | bytes 1568 | tf_op jit(solution)/shard_map/ppermute | solution.py:18
  471.8 3.2 collective-permute-start.45
  472.1 3.0 collective-permute-start.46
  475.2 5.1 collective-permute-start.47
  475.3 6.9 %collective-permute-start.48 = (f32[130,1]{1,0:T(8,128)S(1)}, f32[130,1]{1,0:T(8,128)S(1)}, u32[]{:S(2)}, u32[]{:S(2)}) collective-permute-start(f32[130,1]{1,0:T(8,128)S(1)} %get-tuple-element.116), channel_id=1, source_target_pairs={{0,1},{1,2},{2,3},{3,0},{4,5},{5,6},{6,7},{7,4},{8,9},{9,10},{10,1... | collective-permute-start | bytes 1568 | tf_op jit(solution)/shard_map/ppermute | solution.py:18
  515.7 3.1 collective-permute-start.49
  515.8 3.0 collective-permute-start.50
  518.9 4.8 collective-permute-start.51
  519.3 6.8 %collective-permute-start.52 = (f32[130,1]{1,0:T(8,128)S(1)}, f32[130,1]{1,0:T(8,128)S(1)}, u32[]{:S(2)}, u32[]{:S(2)}) collective-permute-start(f32[130,1]{1,0:T(8,128)S(1)} %get-tuple-element.114), channel_id=1, source_target_pairs={{0,1},{1,2},{2,3},{3,0},{4,5},{5,6},{6,7},{7,4},{8,9},{9,10},{10,1... | collective-permute-start | bytes 1568 | tf_op jit(solution)/shard_map/ppermute | solution.py:18
  561.7 3.1 collective-permute-start.53
  561.8 3.0 collective-permute-start.54
  564.9 4.9 collective-permute-start.55
  565.3 6.9 %collective-permute-start.56 = (f32[130,1]{1,0:T(8,128)S(1)}, f32[130,1]{1,0:T(8,128)S(1)}, u32[]{:S(2)}, u32[]{:S(2)}) collective-permute-start(f32[130,1]{1,0:T(8,128)S(1)} %get-tuple-element.112), channel_id=1, source_target_pairs={{0,1},{1,2},{2,3},{3,0},{4,5},{5,6},{6,7},{7,4},{8,9},{9,10},{10,1... | collective-permute-start | bytes 1568 | tf_op jit(solution)/shard_map/ppermute | solution.py:18
  606.2 3.1 collective-permute-start.57
  606.2 3.0 collective-permute-start.58
  609.4 4.9 collective-permute-start.59
  609.4 6.7 %collective-permute-start.60 = (f32[130,1]{1,0:T(8,128)S(1)}, f32[130,1]{1,0:T(8,128)S(1)}, u32[]{:S(2)}, u32[]{:S(2)}) collective-permute-start(f32[130,1]{1,0:T(8,128)S(1)} %get-tuple-element.110), channel_id=1, source_target_pairs={{0,1},{1,2},{2,3},{3,0},{4,5},{5,6},{6,7},{7,4},{8,9},{9,10},{10,1... | collective-permute-start | bytes 1568 | tf_op jit(solution)/shard_map/ppermute | solution.py:18
where the time goes:
time: 655 us
  blocking collectives  443 us (68%)
  waiting for transfers between devices  91.6 us (14%)
  starting transfers between devices  62.6 us (10%)
  between operations  38.4 us (6%)
  other arithmetic  18.7 us (3%)
    psum x12, blocking collectives, paired(): lax.psum((jnp.sum(residual * residual), jnp.sum(residual * image)), ('lat...  380 us
    psum x2, blocking collectives, coarse_solve(): lax.psum((jnp.sum(source * source), jnp.sum(source * image)), ('lat', 'lo...  62.6 us
    ppermute x30, waiting for transfers between devices, with_halo(): lax.ppermute(lax.slice_in_dim(block, block.shape[dim] - width, None, axis...  48.1 us
    ppermute x30, waiting for transfers between devices, with_halo(): lax.ppermute(lax.slice_in_dim(block, 0, width, axis=dim), axis, backward)  36.5 us
    ppermute x30, starting transfers between devices, with_halo(): lax.ppermute(lax.slice_in_dim(block, 0, width, axis=dim), axis, backward)  34.5 us
    ppermute x30, starting transfers between devices, with_halo(): lax.ppermute(lax.slice_in_dim(block, block.shape[dim] - width, None, axis...  26.8 us
  transfers between devices with their start and end apart: 61, of which 44 were waited for; matrix products, arithmetic and copies ran while one was open for 0% of the time, Pallas kernels for 0%

commit v1 on v0

--- a/solution.py
+++ b/solution.py
@@ -7,6 +7,7 @@
 FINE_ITERS = 2
 COUPLING = 3.0
 EPSILON = 1e-06
+carry_pools = lambda page: lax.psum(lax.psum(page, axis_name="lon"), "lat")
 
 
 def with_halo(block, sides, width):
@@ -68,7 +69,7 @@
 
 
 def paired(residual, image):
-    return lax.psum((jnp.sum(residual * residual), jnp.sum(residual * image)), ("lat", "lon"))
+    return carry_pools((jnp.sum(residual * residual), jnp.sum(residual * image)))
 
 
 def fine_solve(source, faces):

time: 655 us -> 508 us (0.78)
  blocking collectives: 443 us -> 284 us
  waiting for transfers between devices: 91.6 us -> 120 us
  starting transfers between devices: 62.6 us -> 45.9 us
    psum x12 -> x28, blocking collectives: 380 us -> 220 us  [carry_pools = lambda page: lax.psum(lax.psum(page, axis_name='lon'), 'lat')]
    ppermute x30, waiting for transfers between devices: 48.1 us -> 66.5 us  [with_halo(): lax.ppermute(lax.slice_in_dim(block, block.shape[dim] - width, None, axis...]
    ppermute x30, starting transfers between devices: 26.8 us -> 8.93 us  [with_halo(): lax.ppermute(lax.slice_in_dim(block, block.shape[dim] - width, None, axis...]
    ppermute x30, waiting for transfers between devices: 36.5 us -> 44.4 us  [with_halo(): lax.ppermute(lax.slice_in_dim(block, 0, width, axis=dim), axis, backward)]
  transfers between devices with their start and end apart: 61 -> 61, of which waited for: 44 -> 57; matrix products, arithmetic and copies ran while one was open for 0% -> 0% of each run, Pallas kernels for 0% -> 0%
where the time goes in v1:
time: 508 us; the launch traced here: 507 us
  blocking collectives  284 us (56%)
  waiting for transfers between devices  120 us (24%)
  starting transfers between devices  45.9 us (9%)
  between operations  38.3 us (8%)
  other arithmetic  18.7 us (4%)
    psum x28, blocking collectives, carry_pools = lambda page: lax.psum(lax.psum(page, axis_name='lon'), 'lat')  220 us
    ppermute x30, waiting for transfers between devices, with_halo(): lax.ppermute(lax.slice_in_dim(block, block.shape[dim] - width, None, axis...  66.5 us
    psum x2, blocking collectives, coarse_solve(): lax.psum((jnp.sum(source * source), jnp.sum(source * image)), ('lat', 'lo...  63.4 us
    ppermute x30, waiting for transfers between devices, with_halo(): lax.ppermute(lax.slice_in_dim(block, 0, width, axis=dim), axis, backward)  44.4 us
    ppermute x30, starting transfers between devices, with_halo(): lax.ppermute(lax.slice_in_dim(block, 0, width, axis=dim), axis, backward)  35.6 us
    reduce_sum x12, other arithmetic, paired(): jnp.sum(residual * image)  11.5 us
  transfers between devices with their start and end apart: 61, of which 57 were waited for; matrix products, arithmetic and copies ran while one was open for 0% of the time, Pallas kernels for 0%

profile of v1, /device:TPU:0, one launch (start us, length us, event | category | flops | bytes accessed | tf_op | source)
XLA Modules:
  0.0 507.0 jit_solution(1696705771883466837)
XLA Ops:
  0.7 2.4 collective-permute-start.5
  9.1 2.2 collective-permute-start.3
  11.5 1.9 collective-permute-start.6
  13.6 2.3 collective-permute-done.2
  15.8 2.8 collective-permute-done.3
  22.7 10.9 %all-reduce.15 = (f32[]{:T(128)}, f32[]{:T(128)}) all-reduce(f32[]{:T(128)} %get-tuple-element.47, f32[]{:T(128)} %get-tuple-element.22), channel_id=1, replica_groups=mesh['tm'=2,'lat'=4,'lon'=4] {'lon'}, use_global_device_ids=true, to_apply=%region_4.5 | all-reduce | flops 2 | bytes 16 | tf_op jit(solution)/shard_map/psum | solution.py:10
  33.6 6.3 %all-reduce.29 = (f32[]{:T(128)}, f32[]{:T(128)}) all-reduce(f32[]{:T(128)} %get-tuple-element.92, f32[]{:T(128)} %get-tuple-element.93), channel_id=1, replica_groups=mesh['tm'=2,'lat'=4,'lon'=4] {'lat'}, use_global_device_ids=true, to_apply=%region_5.6 | all-reduce | flops 2 | bytes 16 | tf_op jit(solution)/shard_map/psum | solution.py:10
  47.4 2.5 collective-permute-done.10
  52.1 9.9 %all-reduce.14 = (f32[]{:T(128)}, f32[]{:T(128)}) all-reduce(f32[]{:T(128)} %get-tuple-element.61, f32[]{:T(128)} %get-tuple-element.60), channel_id=1, replica_groups=mesh['tm'=2,'lat'=4,'lon'=4] {'lon'}, use_global_device_ids=true, to_apply=%region_10.11 | all-reduce | flops 2 | bytes 16 | tf_op jit(solution)/shard_map/psum | solution.py:10
  61.9 6.3 %all-reduce.28 = (f32[]{:T(128)}, f32[]{:T(128)}) all-reduce(f32[]{:T(128)} %get-tuple-element.90, f32[]{:T(128)} %get-tuple-element.91), channel_id=1, replica_groups=mesh['tm'=2,'lat'=4,'lon'=4] {'lat'}, use_global_device_ids=true, to_apply=%region_11.12 | all-reduce | flops 2 | bytes 16 | tf_op jit(solution)/shard_map/psum | solution.py:10
  77.1 2.3 collective-permute-done.14
  79.4 3.0 collective-permute-done.15
  83.4 9.1 %all-reduce.13 = (f32[]{:T(128)}, f32[]{:T(128)}) all-reduce(f32[]{:T(128)} %get-tuple-element.59, f32[]{:T(128)} %get-tuple-element.58), channel_id=1, replica_groups=mesh['tm'=2,'lat'=4,'lon'=4] {'lon'}, use_global_device_ids=true, to_apply=%region_16.17 | all-reduce | flops 2 | bytes 16 | tf_op jit(solution)/shard_map/psum | solution.py:10
  92.4 6.3 %all-reduce.27 = (f32[]{:T(128)}, f32[]{:T(128)}) all-reduce(f32[]{:T(128)} %get-tuple-element.88, f32[]{:T(128)} %get-tuple-element.89), channel_id=1, replica_groups=mesh['tm'=2,'lat'=4,'lon'=4] {'lat'}, use_global_device_ids=true, to_apply=%region_17.18 | all-reduce | flops 2 | bytes 16 | tf_op jit(solution)/shard_map/psum | solution.py:10
  103.6 2.0 collective-permute-start.18
  108.0 3.8 collective-permute-done.19
  112.7 9.1 %all-reduce.12 = (f32[]{:T(128)}, f32[]{:T(128)}) all-reduce(f32[]{:T(128)} %get-tuple-element.57, f32[]{:T(128)} %get-tuple-element.56), channel_id=1, replica_groups=mesh['tm'=2,'lat'=4,'lon'=4] {'lon'}, use_global_device_ids=true, to_apply=%region_22.23 | all-reduce | flops 2 | bytes 16 | tf_op jit(solution)/shard_map/psum | solution.py:10
  121.8 6.3 %all-reduce.26 = (f32[]{:T(128)}, f32[]{:T(128)}) all-reduce(f32[]{:T(128)} %get-tuple-element.86, f32[]{:T(128)} %get-tuple-element.87), channel_id=1, replica_groups=mesh['tm'=2,'lat'=4,'lon'=4] {'lat'}, use_global_device_ids=true, to_apply=%region_23.24 | all-reduce | flops 2 | bytes 16 | tf_op jit(solution)/shard_map/psum | solution.py:10
  134.9 2.0 collective-permute-start.22
  136.9 2.3 collective-permute-done.22
  139.2 3.8 collective-permute-done.23
  144.0 9.1 %all-reduce.11 = (f32[]{:T(128)}, f32[]{:T(128)}) all-reduce(f32[]{:T(128)} %get-tuple-element.55, f32[]{:T(128)} %get-tuple-element.54), channel_id=1, replica_groups=mesh['tm'=2,'lat'=4,'lon'=4] {'lon'}, use_global_device_ids=true, to_apply=%region_28.29 | all-reduce | flops 2 | bytes 16 | tf_op jit(solution)/shard_map/psum | solution.py:10
  153.0 6.3 %all-reduce.25 = (f32[]{:T(128)}, f32[]{:T(128)}) all-reduce(f32[]{:T(128)} %get-tuple-element.84, f32[]{:T(128)} %get-tuple-element.85), channel_id=1, replica_groups=mesh['tm'=2,'lat'=4,'lon'=4] {'lat'}, use_global_device_ids=true, to_apply=%region_29.30 | all-reduce | flops 2 | bytes 16 | tf_op jit(solution)/shard_map/psum | solution.py:10
  164.2 2.0 collective-permute-start.26
  168.6 3.8 collective-permute-done.27
  173.3 9.1 %all-reduce.10 = (f32[]{:T(128)}, f32[]{:T(128)}) all-reduce(f32[]{:T(128)} %get-tuple-element.53, f32[]{:T(128)} %get-tuple-element.52), channel_id=1, replica_groups=mesh['tm'=2,'lat'=4,'lon'=4] {'lon'}, use_global_device_ids=true, to_apply=%region_34.35 | all-reduce | flops 2 | bytes 16 | tf_op jit(solution)/shard_map/psum | solution.py:10
  182.4 6.3 %all-reduce.24 = (f32[]{:T(128)}, f32[]{:T(128)}) all-reduce(f32[]{:T(128)} %get-tuple-element.82, f32[]{:T(128)} %get-tuple-element.83), channel_id=1, replica_groups=mesh['tm'=2,'lat'=4,'lon'=4] {'lat'}, use_global_device_ids=true, to_apply=%region_35.36 | all-reduce | flops 2 | bytes 16 | tf_op jit(solution)/shard_map/psum | solution.py:10
  195.5 2.0 collective-permute-start.30
  197.5 2.3 collective-permute-done.30
  199.8 3.8 collective-permute-done.31
  204.6 9.1 %all-reduce.9 = (f32[]{:T(128)}, f32[]{:T(128)}) all-reduce(f32[]{:T(128)} %get-tuple-element.51, f32[]{:T(128)} %get-tuple-element.50), channel_id=1, replica_groups=mesh['tm'=2,'lat'=4,'lon'=4] {'lon'}, use_global_device_ids=true, to_apply=%region_40.41 | all-reduce | flops 2 | bytes 16 | tf_op jit(solution)/shard_map/psum | solution.py:10
  213.6 6.3 %all-reduce.23 = (f32[]{:T(128)}, f32[]{:T(128)}) all-reduce(f32[]{:T(128)} %get-tuple-element.80, f32[]{:T(128)} %get-tuple-element.81), channel_id=1, replica_groups=mesh['tm'=2,'lat'=4,'lon'=4] {'lat'}, use_global_device_ids=true, to_apply=%region_41.42 | all-reduce | flops 2 | bytes 16 | tf_op jit(solution)/shard_map/psum | solution.py:10
  224.8 2.0 collective-permute-start.34
  226.9 33.0 %all-reduce.1 = (f32[]{:T(128)}, f32[]{:T(128)}) all-reduce(f32[]{:T(128)} %get-tuple-element.47, f32[]{:T(128)} %get-tuple-element.21), channel_id=1, replica_groups=mesh['tm'=2,'lat'=4,'lon'=4] {'lat','lon'}, use_global_device_ids=true, to_apply=%region_1.2 | all-reduce | flops 2 | bytes 16 | tf_op jit(solution)/shard_map/while/body/eval_jaxpr/psum | solution.py:99
  262.7 9.1 %all-reduce.8 = (f32[]{:T(128)}, f32[]{:T(128)}) all-reduce(f32[]{:T(128)} %get-tuple-element.49, f32[]{:T(128)} %get-tuple-element.48), channel_id=1, replica_groups=mesh['tm'=2,'lat'=4,'lon'=4] {'lon'}, use_global_device_ids=true, to_apply=%region_46.47 | all-reduce | flops 2 | bytes 16 | tf_op jit(solution)/shard_map/psum | solution.py:10
  271.7 6.3 %all-reduce.22 = (f32[]{:T(128)}, f32[]{:T(128)}) all-reduce(f32[]{:T(128)} %get-tuple-element.78, f32[]{:T(128)} %get-tuple-element.79), channel_id=1, replica_groups=mesh['tm'=2,'lat'=4,'lon'=4] {'lat'}, use_global_device_ids=true, to_apply=%region_47.48 | all-reduce | flops 2 | bytes 16 | tf_op jit(solution)/shard_map/psum | solution.py:10
  282.6 8.7 %collective-permute-done.36 = f32[128,512]{1,0:T(8,128)S(1)} collective-permute-done((f32[128,512]{1,0:T(8,128)S(1)}, f32[128,512]{1,0:T(8,128)S(1)}, u32[]{:S(2)}, u32[]{:S(2)}) %collective-permute-start.36) | collective-permute-done | bytes 262176 | tf_op jit(solution)/shard_map/while/body/eval_jaxpr/ppermute | solution.py:30
  294.5 2.1 collective-permute-start.39
  296.6 2.3 collective-permute-done.39
  298.9 3.8 collective-permute-done.40
  303.7 30.4 %all-reduce = (f32[]{:T(128)}, f32[]{:T(128)}) all-reduce(f32[]{:T(128)} %get-tuple-element.25, f32[]{:T(128)} %get-tuple-element.23), channel_id=1, replica_groups=mesh['tm'=2,'lat'=4,'lon'=4] {'lat','lon'}, use_global_device_ids=true, to_apply=%region_52.53 | all-reduce | flops 2 | bytes 16 | tf_op jit(solution)/shard_map/psum | solution.py:99
  334.7 11.2 %all-reduce.7 = (f32[]{:T(128)}, f32[]{:T(128)}) all-reduce(f32[]{:T(128)} %get-tuple-element.25, f32[]{:T(128)} %get-tuple-element.24), channel_id=1, replica_groups=mesh['tm'=2,'lat'=4,'lon'=4] {'lon'}, use_global_device_ids=true, to_apply=%region_55.0 | all-reduce | flops 2 | bytes 16 | tf_op jit(solution)/shard_map/psum | solution.py:10
  345.9 6.4 %all-reduce.21 = (f32[]{:T(128)}, f32[]{:T(128)}) all-reduce(f32[]{:T(128)} %get-tuple-element.76, f32[]{:T(128)} %get-tuple-element.77), channel_id=1, replica_groups=mesh['tm'=2,'lat'=4,'lon'=4] {'lat'}, use_global_device_ids=true, to_apply=%region_56.0 | all-reduce | flops 2 | bytes 16 | tf_op jit(solution)/shard_map/psum | solution.py:10
  358.1 2.0 collective-permute-start.44
  360.8 2.4 collective-permute-done.43
  365.2 9.6 %all-reduce.6 = (f32[]{:T(128)}, f32[]{:T(128)}) all-reduce(f32[]{:T(128)} %get-tuple-element.46, f32[]{:T(128)} %get-tuple-element.45), channel_id=1, replica_groups=mesh['tm'=2,'lat'=4,'lon'=4] {'lon'}, use_global_device_ids=true, to_apply=%region_61.62 | all-reduce | flops 2 | bytes 16 | tf_op jit(solution)/shard_map/psum | solution.py:10
  374.8 6.3 %all-reduce.20 = (f32[]{:T(128)}, f32[]{:T(128)}) all-reduce(f32[]{:T(128)} %get-tuple-element.74, f32[]{:T(128)} %get-tuple-element.75), channel_id=1, replica_groups=mesh['tm'=2,'lat'=4,'lon'=4] {'lat'}, use_global_device_ids=true, to_apply=%region_62.63 | all-reduce | flops 2 | bytes 16 | tf_op jit(solution)/shard_map/psum | solution.py:10
  390.1 2.3 collective-permute-done.47
  392.4 3.3 collective-permute-done.48
  396.7 9.0 %all-reduce.5 = (f32[]{:T(128)}, f32[]{:T(128)}) all-reduce(f32[]{:T(128)} %get-tuple-element.44, f32[]{:T(128)} %get-tuple-element.43), channel_id=1, replica_groups=mesh['tm'=2,'lat'=4,'lon'=4] {'lon'}, use_global_device_ids=true, to_apply=%region_67.68 | all-reduce | flops 2 | bytes 16 | tf_op jit(solution)/shard_map/psum | solution.py:10
  405.7 6.3 %all-reduce.19 = (f32[]{:T(128)}, f32[]{:T(128)}) all-reduce(f32[]{:T(128)} %get-tuple-element.72, f32[]{:T(128)} %get-tuple-element.73), channel_id=1, replica_groups=mesh['tm'=2,'lat'=4,'lon'=4] {'lat'}, use_global_device_ids=true, to_apply=%region_68.69 | all-reduce | flops 2 | bytes 16 | tf_op jit(solution)/shard_map/psum | solution.py:10
  417.2 2.0 collective-permute-start.51
  421.5 3.8 collective-permute-done.52
  426.3 9.0 %all-reduce.4 = (f32[]{:T(128)}, f32[]{:T(128)}) all-reduce(f32[]{:T(128)} %get-tuple-element.42, f32[]{:T(128)} %get-tuple-element.41), channel_id=1, replica_groups=mesh['tm'=2,'lat'=4,'lon'=4] {'lon'}, use_global_device_ids=true, to_apply=%region_73.74 | all-reduce | flops 2 | bytes 16 | tf_op jit(solution)/shard_map/psum | solution.py:10
  435.3 6.3 %all-reduce.18 = (f32[]{:T(128)}, f32[]{:T(128)}) all-reduce(f32[]{:T(128)} %get-tuple-element.70, f32[]{:T(128)} %get-tuple-element.71), channel_id=1, replica_groups=mesh['tm'=2,'lat'=4,'lon'=4] {'lat'}, use_global_device_ids=true, to_apply=%region_74.75 | all-reduce | flops 2 | bytes 16 | tf_op jit(solution)/shard_map/psum | solution.py:10
  448.6 2.0 collective-permute-start.55
  450.6 2.3 collective-permute-done.55
  452.9 3.8 collective-permute-done.56
  457.7 9.0 %all-reduce.3 = (f32[]{:T(128)}, f32[]{:T(128)}) all-reduce(f32[]{:T(128)} %get-tuple-element.40, f32[]{:T(128)} %get-tuple-element.38), channel_id=1, replica_groups=mesh['tm'=2,'lat'=4,'lon'=4] {'lon'}, use_global_device_ids=true, to_apply=%region_79.80 | all-reduce | flops 2 | bytes 16 | tf_op jit(solution)/shard_map/psum | solution.py:10
  466.7 6.3 %all-reduce.17 = (f32[]{:T(128)}, f32[]{:T(128)}) all-reduce(f32[]{:T(128)} %get-tuple-element.68, f32[]{:T(128)} %get-tuple-element.69), channel_id=1, replica_groups=mesh['tm'=2,'lat'=4,'lon'=4] {'lat'}, use_global_device_ids=true, to_apply=%region_80.81 | all-reduce | flops 2 | bytes 16 | tf_op jit(solution)/shard_map/psum | solution.py:10
  478.1 2.0 collective-permute-start.59
  482.5 3.8 collective-permute-done.60
  487.2 9.0 %all-reduce.2 = (f32[]{:T(128)}, f32[]{:T(128)}) all-reduce(f32[]{:T(128)} %get-tuple-element.36, f32[]{:T(128)} %get-tuple-element.26), channel_id=1, replica_groups=mesh['tm'=2,'lat'=4,'lon'=4] {'lon'}, use_global_device_ids=true, to_apply=%region_85.86 | all-reduce | flops 2 | bytes 16 | tf_op jit(solution)/shard_map/psum | solution.py:10
  496.2 6.3 %all-reduce.16 = (f32[]{:T(128)}, f32[]{:T(128)}) all-reduce(f32[]{:T(128)} %get-tuple-element.66, f32[]{:T(128)} %get-tuple-element.67), channel_id=1, replica_groups=mesh['tm'=2,'lat'=4,'lon'=4] {'lat'}, use_global_device_ids=true, to_apply=%region_86.87 | all-reduce | flops 2 | bytes 16 | tf_op jit(solution)/shard_map/psum | solution.py:10
  (161 shorter events, 89.0 us)
Async XLA Ops:
  0.7 10.6 %collective-permute-start.5 = (f32[1,512]{1,0:T(1,128)S(1)}, f32[1,512]{1,0:T(1,128)S(1)}, u32[]{:S(2)}, u32[]{:S(2)}) collective-permute-start(f32[1,512]{1,0:T(1,128)S(1)} %get-tuple-element.195), channel_id=1, source_target_pairs={{4,0},{8,4},{12,8},{0,12},{5,1},{9,5},{13,9},{1,13},{6,2},{10,6},{... | collective-permute-start | bytes 6152 | tf_op jit(solution)/shard_map/while/body/eval_jaxpr/ppermute | solution.py:22
  3.2 1.0 copy-start.2
  3.2 8.2 %collective-permute-start.4 = (f32[1,512]{1,0:T(1,128)S(1)}, f32[1,512]{1,0:T(1,128)S(1)}, u32[]{:S(2)}, u32[]{:S(2)}) collective-permute-start(f32[1,512]{1,0:T(1,128)S(1)} %get-tuple-element.196), channel_id=1, source_target_pairs={{0,4},{4,8},{8,12},{12,0},{1,5},{5,9},{9,13},{13,1},{2,6},{6,10},{... | collective-permute-start | bytes 6152 | tf_op jit(solution)/shard_map/while/body/eval_jaxpr/ppermute | solution.py:19
  4.2 3.1 collective-permute-start
  5.0 2.4 collective-permute-start.1
  6.0 5.3 %copy-start = (f32[1,128,512]{2,1,0:T(8,128)S(1)}, f32[1,128,512]{2,1,0:T(8,128)}, u32[]{:S(2)}) copy-start(f32[1,128,512]{2,1,0:T(8,128)} %param.7) | copy-start | bytes 786436
  7.5 8.3 %collective-permute-start.2 = (f32[2,130,1]{2,1,0:T(8,128)S(1)}, f32[2,130,1]{2,1,0:T(8,128)S(1)}, u32[]{:S(2)}, u32[]{:S(2)}) collective-permute-start(f32[2,130,1]{2,1,0:T(8,128)S(1)} %get-tuple-element.135), channel_id=1, source_target_pairs={{0,1},{1,2},{2,3},{3,0},{4,5},{5,6},{6,7},{7,4},{8,9},{9,10},{10,1... | collective-permute-start | bytes 3128 | tf_op jit(solution)/shard_map/ppermute | solution.py:19
  9.1 9.5 %collective-permute-start.3 = (f32[2,130,1]{2,1,0:T(8,128)S(1)}, f32[2,130,1]{2,1,0:T(8,128)S(1)}, u32[]{:S(2)}, u32[]{:S(2)}) collective-permute-start(f32[2,130,1]{2,1,0:T(8,128)S(1)} %get-tuple-element.136), channel_id=1, source_target_pairs={{1,0},{2,1},{3,2},{0,3},{5,4},{6,5},{7,6},{4,7},{9,8},{10,9},{11,1... | collective-permute-start | bytes 3128 | tf_op jit(solution)/shard_map/ppermute | solution.py:22
  11.5 8.5 %collective-permute-start.6 = (f32[130,1]{1,0:T(8,128)S(1)}, f32[130,1]{1,0:T(8,128)S(1)}, u32[]{:S(2)}, u32[]{:S(2)}) collective-permute-start(f32[130,1]{1,0:T(8,128)S(1)} %get-tuple-element.165), channel_id=1, source_target_pairs={{1,0},{2,1},{3,2},{0,3},{5,4},{6,5},{7,6},{4,7},{9,8},{10,9},{11,1... | collective-permute-start | bytes 1568 | tf_op jit(solution)/shard_map/while/body/eval_jaxpr/ppermute | solution.py:22
  13.3 8.4 %collective-permute-start.7 = (f32[130,1]{1,0:T(8,128)S(1)}, f32[130,1]{1,0:T(8,128)S(1)}, u32[]{:S(2)}, u32[]{:S(2)}) collective-permute-start(f32[130,1]{1,0:T(8,128)S(1)} %get-tuple-element.166), channel_id=1, source_target_pairs={{0,1},{1,2},{2,3},{3,0},{4,5},{5,6},{6,7},{7,4},{8,9},{9,10},{10,1... | collective-permute-start | bytes 1568 | tf_op jit(solution)/shard_map/while/body/eval_jaxpr/ppermute | solution.py:19
  41.1 30.2 %copy-start.1 = (f32[4,128,512]{2,1,0:T(8,128)S(1)}, f32[4,128,512]{2,1,0:T(8,128)}, u32[]{:S(2)}) copy-start(f32[4,128,512]{2,1,0:T(8,128)} %param.4) | copy-start | bytes 3145732
  41.2 1.8 collective-permute-start.9
  41.7 3.0 collective-permute-start.8
  44.8 5.1 %collective-permute-start.10 = (f32[130,1]{1,0:T(8,128)S(1)}, f32[130,1]{1,0:T(8,128)S(1)}, u32[]{:S(2)}, u32[]{:S(2)}) collective-permute-start(f32[130,1]{1,0:T(8,128)S(1)} %get-tuple-element.163), channel_id=1, source_target_pairs={{1,0},{2,1},{3,2},{0,3},{5,4},{6,5},{7,6},{4,7},{9,8},{10,9},{11,1... | collective-permute-start | bytes 1568 | tf_op jit(solution)/shard_map/ppermute | solution.py:22
  45.0 6.1 %collective-permute-start.11 = (f32[130,1]{1,0:T(8,128)S(1)}, f32[130,1]{1,0:T(8,128)S(1)}, u32[]{:S(2)}, u32[]{:S(2)}) collective-permute-start(f32[130,1]{1,0:T(8,128)S(1)} %get-tuple-element.164), channel_id=1, source_target_pairs={{0,1},{1,2},{2,3},{3,0},{4,5},{5,6},{6,7},{7,4},{8,9},{9,10},{10,1... | collective-permute-start | bytes 1568 | tf_op jit(solution)/shard_map/ppermute | solution.py:19
  71.4 1.8 collective-permute-start.13
  71.9 3.0 collective-permute-start.12
  75.0 4.4 collective-permute-start.14
  76.3 6.1 %collective-permute-start.15 = (f32[130,1]{1,0:T(8,128)S(1)}, f32[130,1]{1,0:T(8,128)S(1)}, u32[]{:S(2)}, u32[]{:S(2)}) collective-permute-start(f32[130,1]{1,0:T(8,128)S(1)} %get-tuple-element.162), channel_id=1, source_target_pairs={{0,1},{1,2},{2,3},{3,0},{4,5},{5,6},{6,7},{7,4},{8,9},{9,10},{10,1... | collective-permute-start | bytes 1568 | tf_op jit(solution)/shard_map/ppermute | solution.py:19
  100.0 1.8 collective-permute-start.17
  100.5 3.0 collective-permute-start.16
  103.6 4.4 collective-permute-start.18
  105.6 6.1 %collective-permute-start.19 = (f32[130,1]{1,0:T(8,128)S(1)}, f32[130,1]{1,0:T(8,128)S(1)}, u32[]{:S(2)}, u32[]{:S(2)}) collective-permute-start(f32[130,1]{1,0:T(8,128)S(1)} %get-tuple-element.160), channel_id=1, source_target_pairs={{0,1},{1,2},{2,3},{3,0},{4,5},{5,6},{6,7},{7,4},{8,9},{9,10},{10,1... | collective-permute-start | bytes 1568 | tf_op jit(solution)/shard_map/ppermute | solution.py:19
  131.2 1.9 collective-permute-start.21
  131.8 3.0 collective-permute-start.20
  134.9 4.4 collective-permute-start.22
  136.9 6.1 %collective-permute-start.23 = (f32[130,1]{1,0:T(8,128)S(1)}, f32[130,1]{1,0:T(8,128)S(1)}, u32[]{:S(2)}, u32[]{:S(2)}) collective-permute-start(f32[130,1]{1,0:T(8,128)S(1)} %get-tuple-element.158), channel_id=1, source_target_pairs={{0,1},{1,2},{2,3},{3,0},{4,5},{5,6},{6,7},{7,4},{8,9},{9,10},{10,1... | collective-permute-start | bytes 1568 | tf_op jit(solution)/shard_map/ppermute | solution.py:19
  160.6 1.8 collective-permute-start.25
  161.1 3.0 collective-permute-start.24
  164.2 4.4 collective-permute-start.26
  166.2 6.1 %collective-permute-start.27 = (f32[130,1]{1,0:T(8,128)S(1)}, f32[130,1]{1,0:T(8,128)S(1)}, u32[]{:S(2)}, u32[]{:S(2)}) collective-permute-start(f32[130,1]{1,0:T(8,128)S(1)} %get-tuple-element.156), channel_id=1, source_target_pairs={{0,1},{1,2},{2,3},{3,0},{4,5},{5,6},{6,7},{7,4},{8,9},{9,10},{10,1... | collective-permute-start | bytes 1568 | tf_op jit(solution)/shard_map/ppermute | solution.py:19
  191.8 1.9 collective-permute-start.29
  192.4 3.0 collective-permute-start.28
  195.5 4.4 collective-permute-start.30
  197.5 6.1 %collective-permute-start.31 = (f32[130,1]{1,0:T(8,128)S(1)}, f32[130,1]{1,0:T(8,128)S(1)}, u32[]{:S(2)}, u32[]{:S(2)}) collective-permute-start(f32[130,1]{1,0:T(8,128)S(1)} %get-tuple-element.154), channel_id=1, source_target_pairs={{0,1},{1,2},{2,3},{3,0},{4,5},{5,6},{6,7},{7,4},{8,9},{9,10},{10,1... | collective-permute-start | bytes 1568 | tf_op jit(solution)/shard_map/ppermute | solution.py:19
  221.2 1.8 collective-permute-start.33
  221.7 3.0 collective-permute-start.32
  224.8 36.9 %collective-permute-start.34 = (f32[130,1]{1,0:T(8,128)S(1)}, f32[130,1]{1,0:T(8,128)S(1)}, u32[]{:S(2)}, u32[]{:S(2)}) collective-permute-start(f32[130,1]{1,0:T(8,128)S(1)} %get-tuple-element.151), channel_id=1, source_target_pairs={{1,0},{2,1},{3,2},{0,3},{5,4},{6,5},{7,6},{4,7},{9,8},{10,9},{11,1... | collective-permute-start | bytes 1568 | tf_op jit(solution)/shard_map/ppermute | solution.py:22
  226.8 34.9 %collective-permute-start.35 = (f32[130,1]{1,0:T(8,128)S(1)}, f32[130,1]{1,0:T(8,128)S(1)}, u32[]{:S(2)}, u32[]{:S(2)}) collective-permute-start(f32[130,1]{1,0:T(8,128)S(1)} %get-tuple-element.152), channel_id=1, source_target_pairs={{0,1},{1,2},{2,3},{3,0},{4,5},{5,6},{6,7},{7,4},{8,9},{9,10},{10,1... | collective-permute-start | bytes 1568 | tf_op jit(solution)/shard_map/ppermute | solution.py:19
  281.3 10.0 %collective-permute-start.36 = (f32[128,512]{1,0:T(8,128)S(1)}, f32[128,512]{1,0:T(8,128)S(1)}, u32[]{:S(2)}, u32[]{:S(2)}) collective-permute-start(f32[128,512]{1,0:T(8,128)S(1)} %get-tuple-element.125), channel_id=1, source_target_pairs={{16,0},{17,1},{18,2},{19,3},{20,4},{21,5},{22,6},{23,7},{24,8},{25... | collective-permute-start | bytes 786440 | tf_op jit(solution)/shard_map/while/body/eval_jaxpr/ppermute | solution.py:30
  291.3 1.4 collective-permute-start.38
  291.4 3.1 collective-permute-start.37
  294.5 4.4 collective-permute-start.39
  296.6 6.1 %collective-permute-start.40 = (f32[130,1]{1,0:T(8,128)S(1)}, f32[130,1]{1,0:T(8,128)S(1)}, u32[]{:S(2)}, u32[]{:S(2)}) collective-permute-start(f32[130,1]{1,0:T(8,128)S(1)} %get-tuple-element.150), channel_id=1, source_target_pairs={{0,1},{1,2},{2,3},{3,0},{4,5},{5,6},{6,7},{7,4},{8,9},{9,10},{10,1... | collective-permute-start | bytes 1568 | tf_op jit(solution)/shard_map/ppermute | solution.py:19
  354.3 1.9 collective-permute-start.42
  354.9 3.0 collective-permute-start.41
  358.0 5.1 %collective-permute-start.43 = (f32[130,1]{1,0:T(8,128)S(1)}, f32[130,1]{1,0:T(8,128)S(1)}, u32[]{:S(2)}, u32[]{:S(2)}) collective-permute-start(f32[130,1]{1,0:T(8,128)S(1)} %get-tuple-element.147), channel_id=1, source_target_pairs={{1,0},{2,1},{3,2},{0,3},{5,4},{6,5},{7,6},{4,7},{9,8},{10,9},{11,1... | collective-permute-start | bytes 1568 | tf_op jit(solution)/shard_map/ppermute | solution.py:22
  358.1 6.2 %collective-permute-start.44 = (f32[130,1]{1,0:T(8,128)S(1)}, f32[130,1]{1,0:T(8,128)S(1)}, u32[]{:S(2)}, u32[]{:S(2)}) collective-permute-start(f32[130,1]{1,0:T(8,128)S(1)} %get-tuple-element.148), channel_id=1, source_target_pairs={{0,1},{1,2},{2,3},{3,0},{4,5},{5,6},{6,7},{7,4},{8,9},{9,10},{10,1... | collective-permute-start | bytes 1568 | tf_op jit(solution)/shard_map/ppermute | solution.py:19
  384.5 1.7 collective-permute-start.46
  384.9 3.0 collective-permute-start.45
  388.1 4.4 collective-permute-start.47
  389.6 6.1 %collective-permute-start.48 = (f32[130,1]{1,0:T(8,128)S(1)}, f32[130,1]{1,0:T(8,128)S(1)}, u32[]{:S(2)}, u32[]{:S(2)}) collective-permute-start(f32[130,1]{1,0:T(8,128)S(1)} %get-tuple-element.146), channel_id=1, source_target_pairs={{0,1},{1,2},{2,3},{3,0},{4,5},{5,6},{6,7},{7,4},{8,9},{9,10},{10,1... | collective-permute-start | bytes 1568 | tf_op jit(solution)/shard_map/ppermute | solution.py:19
  413.5 1.9 collective-permute-start.50
  414.1 3.0 collective-permute-start.49
  417.2 4.4 collective-permute-start.51
  419.2 6.1 %collective-permute-start.52 = (f32[130,1]{1,0:T(8,128)S(1)}, f32[130,1]{1,0:T(8,128)S(1)}, u32[]{:S(2)}, u32[]{:S(2)}) collective-permute-start(f32[130,1]{1,0:T(8,128)S(1)} %get-tuple-element.144), channel_id=1, source_target_pairs={{0,1},{1,2},{2,3},{3,0},{4,5},{5,6},{6,7},{7,4},{8,9},{9,10},{10,1... | collective-permute-start | bytes 1568 | tf_op jit(solution)/shard_map/ppermute | solution.py:19
  445.0 1.8 collective-permute-start.54
  445.5 3.0 collective-permute-start.53
  448.6 4.4 collective-permute-start.55
  450.6 6.1 %collective-permute-start.56 = (f32[130,1]{1,0:T(8,128)S(1)}, f32[130,1]{1,0:T(8,128)S(1)}, u32[]{:S(2)}, u32[]{:S(2)}) collective-permute-start(f32[130,1]{1,0:T(8,128)S(1)} %get-tuple-element.142), channel_id=1, source_target_pairs={{0,1},{1,2},{2,3},{3,0},{4,5},{5,6},{6,7},{7,4},{8,9},{9,10},{10,1... | collective-permute-start | bytes 1568 | tf_op jit(solution)/shard_map/ppermute | solution.py:19
  474.5 1.9 collective-permute-start.58
  475.0 3.0 collective-permute-start.57
  478.1 4.4 collective-permute-start.59
  480.2 6.1 %collective-permute-start.60 = (f32[130,1]{1,0:T(8,128)S(1)}, f32[130,1]{1,0:T(8,128)S(1)}, u32[]{:S(2)}, u32[]{:S(2)}) collective-permute-start(f32[130,1]{1,0:T(8,128)S(1)} %get-tuple-element.140), channel_id=1, source_target_pairs={{0,1},{1,2},{2,3},{3,0},{4,5},{5,6},{6,7},{7,4},{8,9},{9,10},{10,1... | collective-permute-start | bytes 1568 | tf_op jit(solution)/shard_map/ppermute | solution.py:19
